TPU v7x, 32 devices: a whole 2x2x4 slice. The times are simulated.
32 devices in a mesh: section: 2 (over x), expert: 16 (over z, y, core).
Axes of the slice: x: 2, y: 2, z: 4, core: 2. Of those that a mesh axis runs over, the one named last changes fastest.
Arguments:
- hidden_in: bfloat16 [2, 128, 3584], P(None, 'expert'), may hold values from -6 to 6
- layer_gain: float32 [2, 3584], P('section'), may hold values from 0.25 to 1.75
- router: bfloat16 [2, 3584, 4], P('section'), may hold values from -0.09375 to 0.09375
- w_gate: bfloat16 [2, 3584, 8192], P('section', None, 'expert'), may hold values from -0.09375 to 0.09375
- w_up: bfloat16 [2, 3584, 8192], P('section', None, 'expert'), may hold values from -0.09375 to 0.09375
- w_down: bfloat16 [2, 8192, 3584], P('section', 'expert'), may hold values from -0.125 to 0.125
- final_gain: float32 [3584], replicated, may hold values from 0.25 to 1.75
- head: bfloat16 [8192, 3584], P(('section', 'expert')), may hold values from -18.775102 to 18.775102
- routing: int32 [2, 2, 128, 2], P('section', None, 'expert'), may hold values from 0 to 3, all different within a row; in each aligned block of 8 rows (0 to 7, 8 to 15, ..., all dimensions but the last counted through in order) at most 4 rows name the same one
- targets: int32 [2, 128], replicated, may hold values from 0 to 8191
- seq_ids: int32 [2, 128], replicated, may hold values from 0 to 3, never falling along the last dimension, each value on 1 to 64 neighbouring positions
Outputs:
- token_logprob: float32 [2, 128], P(None, 'expert')
- seq_mean: float32 [2, 4], replicated
Inputs may be any that keep to these rules, and one draw needn't show every extreme that they name: `routing`: in each aligned block of 8 tokens (the tokens of one device) a token's 2 experts differ and no expert is named by more than 4 tokens; some expert is named by exactly 4. `seq_ids`: ids never fall along a micro-batch's tokens; each of the 4 ids occurs on 1 to 64 tokens, one on exactly 64.
All inputs are finite; a program needn't handle non-finite values.
Results may differ from a plain program's by a relative error of at most 0.014.
Values may be sent and summed in bfloat16 or wider, within the bound.
A program may use at most 64 MiB of HBM per device.

v0:
```python
import jax
import jax.numpy as jnp
from jax import lax
from jax.sharding import PartitionSpec as P

SEQS = 4


def shifted(shard, axis, by):
    size = lax.axis_size(axis)
    pairs = [(i, i + by) for i in range(size) if 0 <= i + by < size]
    return lax.ppermute(shard, axis, pairs)


def broadcast(block, axis, holder):
    block = jnp.where(lax.axis_index(axis) == holder, block, jnp.zeros_like(block))
    return lax.psum(block, axis)


def rms_scale(states, gain):
    values = states.astype(jnp.float32)
    factor = lax.rsqrt(jnp.mean(values * values, -1, keepdims=True) + 1e-06)
    return values * factor * gain


def body(
    hidden_in, layer_gain, router, w_gate, w_up, w_down, final_gain, head, routing, targets, seq_ids
):
    micro_count, tok_count, model_width = hidden_in.shape
    expert_count = router.shape[2]
    top_count = routing.shape[3]
    sections = lax.axis_size("section")
    members = lax.axis_size("expert")
    section_pos = lax.axis_index("section")
    member_pos = lax.axis_index("expert")
    split_count = members // expert_count
    capacity = min(tok_count, 9 * tok_count * top_count // (8 * expert_count))
    tick_count = micro_count + sections - 1

    def expert_rows(incoming):
        sources, slot_count, width_in = incoming.shape
        flat_rows = incoming.reshape(sources * slot_count, width_in)
        gate_val = jnp.dot(flat_rows, w_gate[0], preferred_element_type=jnp.float32)
        up_val = jnp.dot(flat_rows, w_up[0], preferred_element_type=jnp.float32)
        inner = (jax.nn.silu(gate_val) * up_val).astype(jnp.bfloat16)
        partial_value = jnp.dot(inner, w_down[0], preferred_element_type=jnp.float32).astype(
            jnp.bfloat16
        )
        return lax.all_to_all(
            partial_value.reshape(sources, slot_count, width_in),
            "expert",
            split_axis=0,
            concat_axis=0,
            tiled=True,
        )

    def expert_layer(states, micro_pos):
        route_ids = lax.dynamic_index_in_dim(routing[0], micro_pos, 0, keepdims=False)
        normed = rms_scale(states, layer_gain[0]).astype(jnp.bfloat16)
        logits = jnp.dot(normed, router[0], preferred_element_type=jnp.float32)
        chosen = route_ids[:, :, None] == jnp.arange(expert_count, dtype=jnp.int32)[None, None, :]
        affinity = jax.nn.sigmoid(jnp.sum(jnp.where(chosen, logits[:, None, :], 0.0), -1))
        weight = affinity / jnp.sum(affinity, -1, keepdims=True)
        flags = chosen.reshape(tok_count * top_count, expert_count).astype(jnp.int32)
        ranks = jnp.cumsum(flags, 0) - flags
        slot_ids = jnp.sum(ranks * flags, -1).reshape(tok_count, top_count)
        destination = route_ids * capacity + slot_ids
        places = jnp.arange(expert_count * capacity, dtype=jnp.int32)
        table = jnp.any(places[:, None, None] == destination[None], -1).astype(jnp.bfloat16)
        packed = jnp.dot(table, normed, preferred_element_type=jnp.float32).astype(jnp.bfloat16)
        outgoing = jnp.broadcast_to(
            packed.reshape(expert_count, 1, capacity, model_width),
            (expert_count, split_count, capacity, model_width),
        )
        outgoing = outgoing.reshape(members, capacity, model_width)
        returned = expert_rows(
            lax.all_to_all(outgoing, "expert", split_axis=0, concat_axis=0, tiled=True)
        )
        summed = jnp.sum(
            returned.reshape(expert_count, split_count, capacity, model_width).astype(jnp.float32),
            1,
        )
        summed = summed.reshape(expert_count * capacity, model_width)
        picked = summed[destination]
        mixed = jnp.sum(weight[:, :, None] * picked, 1)
        return (states.astype(jnp.float32) + 2.5 * mixed).astype(jnp.bfloat16)

    def advance(step, carry):
        arrived, record = carry
        entering = lax.dynamic_index_in_dim(
            hidden_in, jnp.minimum(step, micro_count - 1), 0, keepdims=False
        )
        states = jnp.where(section_pos == 0, entering, arrived)
        micro_pos = jnp.clip(step - section_pos, 0, micro_count - 1)
        result = expert_layer(states, micro_pos)
        finished = step - (sections - 1)
        record_pos = jnp.clip(finished, 0, micro_count - 1)
        keeping = (finished >= 0) & (section_pos == sections - 1)
        previous = lax.dynamic_index_in_dim(record, record_pos, 0, keepdims=False)
        record = lax.dynamic_update_index_in_dim(
            record, jnp.where(keeping, result, previous), record_pos, 0
        )
        arrived = shifted(result, "section", 1)
        return (arrived, record)

    start_rows = jnp.zeros((tok_count, model_width), jnp.bfloat16)
    start_record = jnp.zeros((micro_count, tok_count, model_width), jnp.bfloat16)
    arrived, record = lax.fori_loop(0, tick_count, advance, (start_rows, start_record))
    shared = broadcast(record, "section", sections - 1)
    normed = rms_scale(lax.all_gather(shared, "expert", axis=1, tiled=True), final_gain).astype(
        jnp.bfloat16
    )
    logits = jnp.einsum("mrd,vd->mrv", normed, head, preferred_element_type=jnp.float32)
    voc_count = head.shape[0]
    vocab_start = (section_pos * members + member_pos) * voc_count
    vocab_ids = vocab_start + jnp.arange(voc_count, dtype=jnp.int32)
    target_hit = targets[:, :, None] == vocab_ids[None, None, :]
    target_part = jnp.sum(jnp.where(target_hit, logits, 0.0), -1)
    local_max = jnp.max(logits, -1)
    peak = lax.pmax(local_max, ("section", "expert"))
    local_sum = jnp.sum(jnp.exp(logits - peak[..., None]), -1)
    total, target_logit = lax.psum((local_sum, target_part), ("section", "expert"))
    logprob = target_logit - (peak + jnp.log(total))
    token_part = lax.dynamic_slice_in_dim(logprob, member_pos * tok_count, tok_count, 1)
    member = seq_ids[:, :, None] == jnp.arange(SEQS, dtype=jnp.int32)[None, None, :]
    sums = jnp.sum(jnp.where(member, logprob[..., None], 0.0), 1)
    counts = jnp.sum(member.astype(jnp.float32), 1)
    return (token_part, sums / counts)


def solution(mesh):
    return jax.shard_map(
        body,
        mesh=mesh,
        in_specs=(
            P(None, "expert", None),
            P("section", None),
            P("section", None, None),
            P("section", None, "expert"),
            P("section", None, "expert"),
            P("section", "expert", None),
            P(),
            P(("section", "expert"), None),
            P("section", None, "expert", None),
            P(),
            P(),
        ),
        out_specs=(P(None, "expert"), P()),
        check_vma=False,
    )
```

profile of v0, /device:TPU:0, one launch (start us, length us, event | category | flops | bytes accessed | tf_op | source)
XLA Modules:
  0.0 332.3 jit_solution(14966221587501759313)
XLA Ops:
  7.3 167.9 %while.17 = (s32[]{:T(128)}, bf16[8,3584]{1,0:T(8,128)(2,1)S(1)}, bf16[2,8,3584]{2,1,0:T(8,128)(2,1)S(1)}, pred[]{:T(512)}, bf16[2,8,3584]{2,1,0:T(8,128)(2,1)},...) while((s32[]{:T(128)}, bf16[8,3584]{1,0:T(8,128)(2,1)S(1)}, ...), condition=%wide.region_9.10_spmd, body=%wide.region_0.9_spmd.sunk | while | flops 707251328 | bytes 21631636 | solution.py:108
  7.3 0.8 constant_dynamic-slice_fusion.6
  9.5 1.0 fusion.70
  10.5 0.8 reduce.2
  11.5 0.9 broadcast_in_dim.134
  12.4 7.4 %all-to-all-start = ((bf16[16,4,3584]{2,1,0:T(4,128)(2,1)}), bf16[16,4,3584]{2,1,0:T(4,128)(2,1)S(1)}, u32[]{:S(2)}, u32[]{:S(2)}) async-start(bf16[16,4,3584]{2,1,0:T(4,128)(2,1)} %bitcast.77), calls=%async_computation | async-start | bytes 917504 | tf_op jit(solution)/shard_map/while/body/eval_jaxpr/all_to_all | solution.py:77
  21.5 0.9 fusion.72
  22.5 10.5 %all-to-all-done = bf16[16,4,3584]{2,1,0:T(4,128)(2,1)S(1)} async-done(((bf16[16,4,3584]{2,1,0:T(4,128)(2,1)}), bf16[16,4,3584]{2,1,0:T(4,128)(2,1)S(1)}, u32[]{:S(2)}, u32[]{:S(2)}) %all-to-all-start) | async-done | bytes 458784 | tf_op jit(solution)/shard_map/while/body/eval_jaxpr/all_to_all | solution.py:77
  33.2 2.8 fusion.71
  35.9 4.6 %convolution_convert_fusion.5 = bf16[64,3584]{1,0:T(8,128)(2,1)S(1)} fusion(bf16[1,512,3584]{2,1,0:T(8,128)(2,1)} %get-tuple-element.450, bf16[64,3584]{1,0:T(8,128)(2,1)S(1)} %reshape.218, bf16[1,3584,512]{2,1,0:T(8,128)(2,1)} %get-tuple-element.449, f32[64,512]{1,0:T(8,128)S(1)} %fusion.71), kind=kOutput, calls=%fused_computation.1.clone.1 | convolution fusion | flops 470188032 | bytes 8388608 | tf_op jit(solution)/shard_map/while/body/eval_jaxpr/dot_general | solution.py:46
  40.6 0.9 reshape.219
  41.4 3.8 %all-to-all-start.1 = ((bf16[16,4,3584]{2,1,0:T(4,128)(2,1)}), bf16[16,4,3584]{2,1,0:T(4,128)(2,1)S(1)}, u32[]{:S(2)}, u32[]{:S(2)}) async-start(bf16[16,4,3584]{2,1,0:T(4,128)(2,1)} %reshape.219), calls=%async_computation.1 | async-start | bytes 917504 | tf_op jit(solution)/shard_map/while/body/eval_jaxpr/all_to_all | solution.py:49
  45.4 13.1 %all-to-all-done.1 = bf16[16,4,3584]{2,1,0:T(4,128)(2,1)S(1)} async-done(((bf16[16,4,3584]{2,1,0:T(4,128)(2,1)}), bf16[16,4,3584]{2,1,0:T(4,128)(2,1)S(1)}, u32[]{:S(2)}, u32[]{:S(2)}) %all-to-all-start.1) | async-done | bytes 458784 | tf_op jit(solution)/shard_map/while/body/eval_jaxpr/all_to_all | solution.py:49
  59.9 3.4 %collective-permute-start = (bf16[8,3584]{1,0:T(8,128)(2,1)S(1)}, bf16[8,3584]{1,0:T(8,128)(2,1)S(1)}, u32[]{:S(2)}, u32[]{:S(2)}) collective-permute-start(bf16[8,3584]{1,0:T(8,128)(2,1)S(1)} %get-tuple-element.401), channel_id=1, source_target_pairs={{0,16},{1,17},{2,18},{3,19},{4,20},{5,21},{6,22},{7,23},{8,24},{9,... | collective-permute-start | bytes 172040 | tf_op jit(solution)/shard_map/while/body/eval_jaxpr/ppermute | solution.py:12
  63.4 1.8 collective-permute-done
  67.2 1.0 fusion.70
  68.2 0.8 reduce.2
  69.3 0.9 broadcast_in_dim.134
  70.1 3.8 %all-to-all-start = ((bf16[16,4,3584]{2,1,0:T(4,128)(2,1)}), bf16[16,4,3584]{2,1,0:T(4,128)(2,1)S(1)}, u32[]{:S(2)}, u32[]{:S(2)}) async-start(bf16[16,4,3584]{2,1,0:T(4,128)(2,1)} %bitcast.77), calls=%async_computation | async-start | bytes 917504 | tf_op jit(solution)/shard_map/while/body/eval_jaxpr/all_to_all | solution.py:77
  75.6 0.9 fusion.72
  76.6 10.5 %all-to-all-done = bf16[16,4,3584]{2,1,0:T(4,128)(2,1)S(1)} async-done(((bf16[16,4,3584]{2,1,0:T(4,128)(2,1)}), bf16[16,4,3584]{2,1,0:T(4,128)(2,1)S(1)}, u32[]{:S(2)}, u32[]{:S(2)}) %all-to-all-start) | async-done | bytes 458784 | tf_op jit(solution)/shard_map/while/body/eval_jaxpr/all_to_all | solution.py:77
  87.3 2.8 fusion.71
  90.1 4.6 %convolution_convert_fusion.5 = bf16[64,3584]{1,0:T(8,128)(2,1)S(1)} fusion(bf16[1,512,3584]{2,1,0:T(8,128)(2,1)} %get-tuple-element.450, bf16[64,3584]{1,0:T(8,128)(2,1)S(1)} %reshape.218, bf16[1,3584,512]{2,1,0:T(8,128)(2,1)} %get-tuple-element.449, f32[64,512]{1,0:T(8,128)S(1)} %fusion.71), kind=kOutput, calls=%fused_computation.1.clone.1 | convolution fusion | flops 470188032 | bytes 8388608 | tf_op jit(solution)/shard_map/while/body/eval_jaxpr/dot_general | solution.py:46
  94.7 0.9 reshape.219
  95.6 3.8 %all-to-all-start.1 = ((bf16[16,4,3584]{2,1,0:T(4,128)(2,1)}), bf16[16,4,3584]{2,1,0:T(4,128)(2,1)S(1)}, u32[]{:S(2)}, u32[]{:S(2)}) async-start(bf16[16,4,3584]{2,1,0:T(4,128)(2,1)} %reshape.219), calls=%async_computation.1 | async-start | bytes 917504 | tf_op jit(solution)/shard_map/while/body/eval_jaxpr/all_to_all | solution.py:49
  99.5 13.1 %all-to-all-done.1 = bf16[16,4,3584]{2,1,0:T(4,128)(2,1)S(1)} async-done(((bf16[16,4,3584]{2,1,0:T(4,128)(2,1)}), bf16[16,4,3584]{2,1,0:T(4,128)(2,1)S(1)}, u32[]{:S(2)}, u32[]{:S(2)}) %all-to-all-start.1) | async-done | bytes 458784 | tf_op jit(solution)/shard_map/while/body/eval_jaxpr/all_to_all | solution.py:49
  114.1 4.3 %collective-permute-start = (bf16[8,3584]{1,0:T(8,128)(2,1)S(1)}, bf16[8,3584]{1,0:T(8,128)(2,1)S(1)}, u32[]{:S(2)}, u32[]{:S(2)}) collective-permute-start(bf16[8,3584]{1,0:T(8,128)(2,1)S(1)} %get-tuple-element.401), channel_id=1, source_target_pairs={{0,16},{1,17},{2,18},{3,19},{4,20},{5,21},{6,22},{7,23},{8,24},{9,... | collective-permute-start | bytes 172040 | tf_op jit(solution)/shard_map/while/body/eval_jaxpr/ppermute | solution.py:12
  118.4 1.8 collective-permute-done
  121.5 0.7 multiply_add_fusion.2
  122.3 1.0 fusion.70
  123.2 0.8 reduce.2
  124.3 0.9 broadcast_in_dim.134
  125.2 3.8 %all-to-all-start = ((bf16[16,4,3584]{2,1,0:T(4,128)(2,1)}), bf16[16,4,3584]{2,1,0:T(4,128)(2,1)S(1)}, u32[]{:S(2)}, u32[]{:S(2)}) async-start(bf16[16,4,3584]{2,1,0:T(4,128)(2,1)} %bitcast.77), calls=%async_computation | async-start | bytes 917504 | tf_op jit(solution)/shard_map/while/body/eval_jaxpr/all_to_all | solution.py:77
  130.7 0.9 fusion.72
  131.7 10.5 %all-to-all-done = bf16[16,4,3584]{2,1,0:T(4,128)(2,1)S(1)} async-done(((bf16[16,4,3584]{2,1,0:T(4,128)(2,1)}), bf16[16,4,3584]{2,1,0:T(4,128)(2,1)S(1)}, u32[]{:S(2)}, u32[]{:S(2)}) %all-to-all-start) | async-done | bytes 458784 | tf_op jit(solution)/shard_map/while/body/eval_jaxpr/all_to_all | solution.py:77
  142.3 2.8 fusion.71
  145.1 4.6 %convolution_convert_fusion.5 = bf16[64,3584]{1,0:T(8,128)(2,1)S(1)} fusion(bf16[1,512,3584]{2,1,0:T(8,128)(2,1)} %get-tuple-element.450, bf16[64,3584]{1,0:T(8,128)(2,1)S(1)} %reshape.218, bf16[1,3584,512]{2,1,0:T(8,128)(2,1)} %get-tuple-element.449, f32[64,512]{1,0:T(8,128)S(1)} %fusion.71), kind=kOutput, calls=%fused_computation.1.clone.1 | convolution fusion | flops 470188032 | bytes 8388608 | tf_op jit(solution)/shard_map/while/body/eval_jaxpr/dot_general | solution.py:46
  149.7 0.9 reshape.219
  150.6 3.8 %all-to-all-start.1 = ((bf16[16,4,3584]{2,1,0:T(4,128)(2,1)}), bf16[16,4,3584]{2,1,0:T(4,128)(2,1)S(1)}, u32[]{:S(2)}, u32[]{:S(2)}) async-start(bf16[16,4,3584]{2,1,0:T(4,128)(2,1)} %reshape.219), calls=%async_computation.1 | async-start | bytes 917504 | tf_op jit(solution)/shard_map/while/body/eval_jaxpr/all_to_all | solution.py:49
  154.5 13.1 %all-to-all-done.1 = bf16[16,4,3584]{2,1,0:T(4,128)(2,1)S(1)} async-done(((bf16[16,4,3584]{2,1,0:T(4,128)(2,1)}), bf16[16,4,3584]{2,1,0:T(4,128)(2,1)S(1)}, u32[]{:S(2)}, u32[]{:S(2)}) %all-to-all-start.1) | async-done | bytes 458784 | tf_op jit(solution)/shard_map/while/body/eval_jaxpr/all_to_all | solution.py:49
  169.1 4.3 %collective-permute-start = (bf16[8,3584]{1,0:T(8,128)(2,1)S(1)}, bf16[8,3584]{1,0:T(8,128)(2,1)S(1)}, u32[]{:S(2)}, u32[]{:S(2)}) collective-permute-start(bf16[8,3584]{1,0:T(8,128)(2,1)S(1)} %get-tuple-element.401), channel_id=1, source_target_pairs={{0,16},{1,17},{2,18},{3,19},{4,20},{5,21},{6,22},{7,23},{8,24},{9,... | collective-permute-start | bytes 172040 | tf_op jit(solution)/shard_map/while/body/eval_jaxpr/ppermute | solution.py:12
  173.4 1.8 collective-permute-done
  175.9 21.4 %all-reduce.3.cloned.1.call-done = bf16[2,8,3584]{2,1,0:T(8,128)(2,1)} async-done(((bf16[2,8,3584]{2,1,0:T(8,128)(2,1)}), bf16[2,8,3584]{2,1,0:T(8,128)(2,1)}) %all-reduce.3.cloned.1.call-update) | async-done | bytes 114704 | tf_op jit(solution)/shard_map/psum | solution.py:17
  197.5 42.9 %all-gather.2.cloned.1.call-done = bf16[2,128,3584]{2,1,0:T(8,128)(2,1)} async-done(((bf16[2,8,3584]{2,1,0:T(8,128)(2,1)}), bf16[2,128,3584]{2,1,0:T(8,128)(2,1)}) %all-gather.2.cloned.1.call-update) | async-done | bytes 1835024 | tf_op jit(solution)/shard_map/all_gather | solution.py:110
  240.4 1.9 fusion.30
  242.4 2.3 fusion.39
  244.6 38.4 %pmax.7 = f32[2,128]{1,0:T(2,128)S(1)} all-reduce(f32[2,128]{1,0:T(2,128)S(1)} %get-tuple-element.314), channel_id=1, replica_groups=mesh['section'=2,'expert'=16] {'section','expert'}, use_global_device_ids=true, to_apply=%region_15.16 | all-reduce | flops 256 | bytes 2048 | tf_op jit(solution)/shard_map/pmax | solution.py:120
  283.3 40.9 %all-reduce = (f32[2,128]{1,0:T(2,128)S(1)}, f32[2,128]{1,0:T(2,128)S(1)}) all-reduce(f32[2,128]{1,0:T(2,128)S(1)} %get-tuple-element.279, f32[2,128]{1,0:T(2,128)S(1)} %get-tuple-element.278), channel_id=1, replica_groups=mesh['section'=2,'expert'=16] {'section','expert'}, use_global_device_ids=true, to_apply=%region_13.14 | all-reduce | flops 512 | bytes 4096 | tf_op jit(solution)/shard_map/psum | solution.py:122
  (116 shorter events, 18.3 us)
Async XLA Ops:
  7.2 235.2 %copy-start = (bf16[256,3584]{1,0:T(8,128)(2,1)S(1)}, bf16[256,3584]{1,0:T(8,128)(2,1)}, u32[]{:S(2)}) copy-start(bf16[256,3584]{1,0:T(8,128)(2,1)} %param.20) | copy-start | bytes 5505028
  7.2 190.2 %all-reduce.3.cloned.1.call-start = ((), (), s32[]{:S(2)}) async-start(), calls=%async_computation.2 | async-start | bytes 229376 | tf_op jit(solution)/shard_map/psum | solution.py:17
  7.3 235.1 %copy-start.3 = (f32[3584]{0:T(1024)S(1)}, f32[3584]{0:T(1024)}, u32[]{:S(2)}) copy-start(f32[3584]{0:T(1024)} %param.19) | copy-start | bytes 43012
  12.4 20.6 %all-to-all-start = ((bf16[16,4,3584]{2,1,0:T(4,128)(2,1)}), bf16[16,4,3584]{2,1,0:T(4,128)(2,1)S(1)}, u32[]{:S(2)}, u32[]{:S(2)}) async-start(bf16[16,4,3584]{2,1,0:T(4,128)(2,1)} %bitcast.77), calls=%async_computation | async-start | bytes 917504 | tf_op jit(solution)/shard_map/while/body/eval_jaxpr/all_to_all | solution.py:77
  41.4 17.0 %all-to-all-start.1 = ((bf16[16,4,3584]{2,1,0:T(4,128)(2,1)}), bf16[16,4,3584]{2,1,0:T(4,128)(2,1)S(1)}, u32[]{:S(2)}, u32[]{:S(2)}) async-start(bf16[16,4,3584]{2,1,0:T(4,128)(2,1)} %reshape.219), calls=%async_computation.1 | async-start | bytes 917504 | tf_op jit(solution)/shard_map/while/body/eval_jaxpr/all_to_all | solution.py:49
  59.9 5.2 %collective-permute-start = (bf16[8,3584]{1,0:T(8,128)(2,1)S(1)}, bf16[8,3584]{1,0:T(8,128)(2,1)S(1)}, u32[]{:S(2)}, u32[]{:S(2)}) collective-permute-start(bf16[8,3584]{1,0:T(8,128)(2,1)S(1)} %get-tuple-element.401), channel_id=1, source_target_pairs={{0,16},{1,17},{2,18},{3,19},{4,20},{5,21},{6,22},{7,23},{8,24},{9,... | collective-permute-start | bytes 172040 | tf_op jit(solution)/shard_map/while/body/eval_jaxpr/ppermute | solution.py:12
  70.1 17.0 %all-to-all-start = ((bf16[16,4,3584]{2,1,0:T(4,128)(2,1)}), bf16[16,4,3584]{2,1,0:T(4,128)(2,1)S(1)}, u32[]{:S(2)}, u32[]{:S(2)}) async-start(bf16[16,4,3584]{2,1,0:T(4,128)(2,1)} %bitcast.77), calls=%async_computation | async-start | bytes 917504 | tf_op jit(solution)/shard_map/while/body/eval_jaxpr/all_to_all | solution.py:77
  95.6 17.0 %all-to-all-start.1 = ((bf16[16,4,3584]{2,1,0:T(4,128)(2,1)}), bf16[16,4,3584]{2,1,0:T(4,128)(2,1)S(1)}, u32[]{:S(2)}, u32[]{:S(2)}) async-start(bf16[16,4,3584]{2,1,0:T(4,128)(2,1)} %reshape.219), calls=%async_computation.1 | async-start | bytes 917504 | tf_op jit(solution)/shard_map/while/body/eval_jaxpr/all_to_all | solution.py:49
  114.1 6.1 %collective-permute-start = (bf16[8,3584]{1,0:T(8,128)(2,1)S(1)}, bf16[8,3584]{1,0:T(8,128)(2,1)S(1)}, u32[]{:S(2)}, u32[]{:S(2)}) collective-permute-start(bf16[8,3584]{1,0:T(8,128)(2,1)S(1)} %get-tuple-element.401), channel_id=1, source_target_pairs={{0,16},{1,17},{2,18},{3,19},{4,20},{5,21},{6,22},{7,23},{8,24},{9,... | collective-permute-start | bytes 172040 | tf_op jit(solution)/shard_map/while/body/eval_jaxpr/ppermute | solution.py:12
  125.2 17.0 %all-to-all-start = ((bf16[16,4,3584]{2,1,0:T(4,128)(2,1)}), bf16[16,4,3584]{2,1,0:T(4,128)(2,1)S(1)}, u32[]{:S(2)}, u32[]{:S(2)}) async-start(bf16[16,4,3584]{2,1,0:T(4,128)(2,1)} %bitcast.77), calls=%async_computation | async-start | bytes 917504 | tf_op jit(solution)/shard_map/while/body/eval_jaxpr/all_to_all | solution.py:77
  150.6 17.0 %all-to-all-start.1 = ((bf16[16,4,3584]{2,1,0:T(4,128)(2,1)}), bf16[16,4,3584]{2,1,0:T(4,128)(2,1)S(1)}, u32[]{:S(2)}, u32[]{:S(2)}) async-start(bf16[16,4,3584]{2,1,0:T(4,128)(2,1)} %reshape.219), calls=%async_computation.1 | async-start | bytes 917504 | tf_op jit(solution)/shard_map/while/body/eval_jaxpr/all_to_all | solution.py:49
  169.1 6.1 %collective-permute-start = (bf16[8,3584]{1,0:T(8,128)(2,1)S(1)}, bf16[8,3584]{1,0:T(8,128)(2,1)S(1)}, u32[]{:S(2)}, u32[]{:S(2)}) collective-permute-start(bf16[8,3584]{1,0:T(8,128)(2,1)S(1)} %get-tuple-element.401), channel_id=1, source_target_pairs={{0,16},{1,17},{2,18},{3,19},{4,20},{5,21},{6,22},{7,23},{8,24},{9,... | collective-permute-start | bytes 172040 | tf_op jit(solution)/shard_map/while/body/eval_jaxpr/ppermute | solution.py:12
  175.9 64.5 %all-gather.2.cloned.1.call-start = ((), (), s32[]{:S(2)}) async-start(), calls=%async_computation.3 | async-start | bytes 1949696 | tf_op jit(solution)/shard_map/all_gather | solution.py:110
  197.4 85.6 %copy-start.1 = (s32[2,128]{1,0:T(2,128)S(1)}, s32[2,128]{1,0:T(2,128)}, u32[]{:S(2)}) copy-start(s32[2,128]{1,0:T(2,128)} %param.22) | copy-start | bytes 3076
  197.4 126.7 %copy-start.2 = (s32[2,128]{1,0:T(2,128)S(1)}, s32[2,128]{1,0:T(2,128)}, u32[]{:S(2)}) copy-start(s32[2,128]{1,0:T(2,128)} %param.23) | copy-start | bytes 3076
Sparse Core Ops, SparseCore 0:
  176.0 21.3 all-reduce.2
  199.7 40.6 all-gather.1
where the time goes:
time: 334 us; the launch traced here: 332 us
  waiting for transfers between devices  141 us (42%)
  blocking collectives  79.3 us (24%)
  starting transfers between devices  38.5 us (12%)
  matrix products  28 us (8%)
  other arithmetic  16 us (5%)
  local copies, waits for them, and re-layouts  15.4 us (5%)
  between operations  14.1 us (4%)
    all_gather x1, waiting for transfers between devices, body(): lax.all_gather(shared, 'expert', axis=1, tiled=True)  42.9 us
    psum x1, blocking collectives, body(): lax.psum((local_sum, target_part), ('section', 'expert'))  40.9 us
    all_to_all x3, waiting for transfers between devices, expert_rows(): lax.all_to_all(partial_value.reshape(sources, slot_count, width_in), 'exp...  39.2 us
    pmax x1, blocking collectives, body(): peak = lax.pmax(local_max, ('section', 'expert'))  38.4 us
    all_to_all x3, waiting for transfers between devices, expert_layer(): lax.all_to_all(outgoing, 'expert', split_axis=0, concat_axis=0, tiled=True)  31.6 us
    psum x1, waiting for transfers between devices, broadcast(): return lax.psum(block, axis)  21.4 us
    all_to_all x3, starting transfers between devices, expert_layer(): lax.all_to_all(outgoing, 'expert', split_axis=0, concat_axis=0, tiled=True)  15 us
    dot_general x3, matrix products, expert_rows(): jnp.dot(inner, w_down[0], preferred_element_type=jnp.float32)  13.8 us
  transfers between devices with their start and end apart: 11, of which 11 were waited for; matrix products, arithmetic and copies ran while one was open for 3% of the time, Pallas kernels for 0%

commit v1 on v0

--- a/solution.py
+++ b/solution.py
@@ -1,9 +1,33 @@
+import functools
 import jax
 import jax.numpy as jnp
 from jax import lax
 from jax.sharding import PartitionSpec as P
 
 SEQS = 4
+
+
+def clear_the_space(shard_in, along_axis):
+    v_next, prior, y2 = (lax.axis_size(along_axis), lax.axis_index(along_axis), shard_in.shape[1])
+    outcome_arr, part_next = (shard_in, 1)
+    while part_next < v_next:
+        outcome_arr = jnp.concatenate(
+            [
+                outcome_arr,
+                lax.ppermute(
+                    outcome_arr,
+                    along_axis,
+                    tuple(((j0, (j0 - part_next) % v_next) for j0 in range(v_next))),
+                ),
+            ],
+            axis=1,
+        )
+        part_next = 2 * part_next
+    spare = jnp.roll(outcome_arr, shift=prior * y2, axis=1)
+    return spare
+
+
+perform_hubs = functools.partial(clear_the_space, along_axis="expert")
 
 
 def shifted(shard, axis, by):
@@ -107,9 +131,7 @@
     start_record = jnp.zeros((micro_count, tok_count, model_width), jnp.bfloat16)
     arrived, record = lax.fori_loop(0, tick_count, advance, (start_rows, start_record))
     shared = broadcast(record, "section", sections - 1)
-    normed = rms_scale(lax.all_gather(shared, "expert", axis=1, tiled=True), final_gain).astype(
-        jnp.bfloat16
-    )
+    normed = rms_scale(perform_hubs(shared), final_gain).astype(jnp.bfloat16)
     logits = jnp.einsum("mrd,vd->mrv", normed, head, preferred_element_type=jnp.float32)
     voc_count = head.shape[0]
     vocab_start = (section_pos * members + member_pos) * voc_count

time: 334 us -> 359 us (1.075)
  waiting for transfers between devices: 141 us -> 158 us
  starting transfers between devices: 38.5 us -> 45.1 us
    ppermute x0 -> x4, waiting for transfers between devices: none -> 60.4 us  [clear_the_space(): lax.ppermute(outcome_arr, along_axis, tuple(((j0, (j0 - part_next) % v_ne...]
    all_gather x1 -> x0, waiting for transfers between devices: 42.9 us -> none  [body(): lax.all_gather(shared, 'expert', axis=1, tiled=True)]
    ppermute x0 -> x4, starting transfers between devices: none -> 6.73 us  [clear_the_space(): lax.ppermute(outcome_arr, along_axis, tuple(((j0, (j0 - part_next) % v_ne...]
  transfers between devices with their start and end apart: 11 -> 14, of which waited for: 11 -> 14; matrix products, arithmetic and copies ran while one was open for 3% -> 3% of each run, Pallas kernels for 0% -> 0%
where the time goes in v1:
time: 359 us; the launch traced here: 357 us
  waiting for transfers between devices  158 us (44%)
  blocking collectives  78.9 us (22%)
  starting transfers between devices  45.1 us (13%)
  matrix products  26.5 us (7%)
  other arithmetic  17.3 us (5%)
  local copies, waits for them, and re-layouts  16.6 us (5%)
  between operations  14.2 us (4%)
    ppermute x4, waiting for transfers between devices, clear_the_space(): lax.ppermute(outcome_arr, along_axis, tuple(((j0, (j0 - part_next) % v_ne...  60.4 us
    psum x1, blocking collectives, body(): lax.psum((local_sum, target_part), ('section', 'expert'))  41.5 us
    all_to_all x3, waiting for transfers between devices, expert_rows(): lax.all_to_all(partial_value.reshape(sources, slot_count, width_in), 'exp...  39.2 us
    pmax x1, blocking collectives, body(): peak = lax.pmax(local_max, ('section', 'expert'))  37.3 us
    all_to_all x3, waiting for transfers between devices, expert_layer(): lax.all_to_all(outgoing, 'expert', split_axis=0, concat_axis=0, tiled=True)  31.6 us
    psum x1, waiting for transfers between devices, broadcast(): return lax.psum(block, axis)  21.5 us
    all_to_all x3, starting transfers between devices, expert_layer(): lax.all_to_all(outgoing, 'expert', split_axis=0, concat_axis=0, tiled=True)  15 us
    dot_general x3, matrix products, expert_rows(): jnp.dot(inner, w_down[0], preferred_element_type=jnp.float32)  13.8 us
  transfers between devices with their start and end apart: 14, of which 14 were waited for; matrix products, arithmetic and copies ran while one was open for 3% of the time, Pallas kernels for 0%

profile of v1, /device:TPU:0, one launch (start us, length us, event | category | flops | bytes accessed | tf_op | source)
XLA Modules:
  0.0 357.1 jit_solution(2149404871257475565)
XLA Ops:
  7.3 168.0 %while.17 = (s32[]{:T(128)}, bf16[8,3584]{1,0:T(8,128)(2,1)S(1)}, bf16[2,8,3584]{2,1,0:T(8,128)(2,1)S(1)}, pred[]{:T(512)}, bf16[2,8,3584]{2,1,0:T(8,128)(2,1)},...) while((s32[]{:T(128)}, bf16[8,3584]{1,0:T(8,128)(2,1)S(1)}, ...), condition=%wide.region_9.10_spmd, body=%wide.region_0.9_spmd.sunk | while | flops 707251328 | bytes 21631636 | solution.py:132
  9.5 1.0 fusion.72
  11.5 0.9 broadcast_in_dim.134
  12.4 7.4 %all-to-all-start = ((bf16[16,4,3584]{2,1,0:T(4,128)(2,1)}), bf16[16,4,3584]{2,1,0:T(4,128)(2,1)S(1)}, u32[]{:S(2)}, u32[]{:S(2)}) async-start(bf16[16,4,3584]{2,1,0:T(4,128)(2,1)} %bitcast.77), calls=%async_computation | async-start | bytes 917504 | tf_op jit(solution)/shard_map/while/body/eval_jaxpr/all_to_all | solution.py:101
  21.5 0.9 fusion.74
  22.5 10.5 %all-to-all-done = bf16[16,4,3584]{2,1,0:T(4,128)(2,1)S(1)} async-done(((bf16[16,4,3584]{2,1,0:T(4,128)(2,1)}), bf16[16,4,3584]{2,1,0:T(4,128)(2,1)S(1)}, u32[]{:S(2)}, u32[]{:S(2)}) %all-to-all-start) | async-done | bytes 458784 | tf_op jit(solution)/shard_map/while/body/eval_jaxpr/all_to_all | solution.py:101
  33.1 2.8 fusion.73
  35.9 4.6 %convolution_convert_fusion.5 = bf16[64,3584]{1,0:T(8,128)(2,1)S(1)} fusion(bf16[1,512,3584]{2,1,0:T(8,128)(2,1)} %get-tuple-element.450, bf16[64,3584]{1,0:T(8,128)(2,1)S(1)} %reshape.218, bf16[1,3584,512]{2,1,0:T(8,128)(2,1)} %get-tuple-element.449, f32[64,512]{1,0:T(8,128)S(1)} %fusion.73), kind=kOutput, calls=%fused_computation.1.clone.1 | convolution fusion | flops 470188032 | bytes 8388608 | tf_op jit(solution)/shard_map/while/body/eval_jaxpr/dot_general | solution.py:70
  41.4 3.8 %all-to-all-start.1 = ((bf16[16,4,3584]{2,1,0:T(4,128)(2,1)}), bf16[16,4,3584]{2,1,0:T(4,128)(2,1)S(1)}, u32[]{:S(2)}, u32[]{:S(2)}) async-start(bf16[16,4,3584]{2,1,0:T(4,128)(2,1)} %reshape.219), calls=%async_computation.1 | async-start | bytes 917504 | tf_op jit(solution)/shard_map/while/body/eval_jaxpr/all_to_all | solution.py:73
  45.4 13.1 %all-to-all-done.1 = bf16[16,4,3584]{2,1,0:T(4,128)(2,1)S(1)} async-done(((bf16[16,4,3584]{2,1,0:T(4,128)(2,1)}), bf16[16,4,3584]{2,1,0:T(4,128)(2,1)S(1)}, u32[]{:S(2)}, u32[]{:S(2)}) %all-to-all-start.1) | async-done | bytes 458784 | tf_op jit(solution)/shard_map/while/body/eval_jaxpr/all_to_all | solution.py:73
  59.9 3.4 collective-permute-start
  63.4 1.8 collective-permute-done
  67.2 1.0 fusion.72
  69.3 0.9 broadcast_in_dim.134
  70.1 3.8 %all-to-all-start = ((bf16[16,4,3584]{2,1,0:T(4,128)(2,1)}), bf16[16,4,3584]{2,1,0:T(4,128)(2,1)S(1)}, u32[]{:S(2)}, u32[]{:S(2)}) async-start(bf16[16,4,3584]{2,1,0:T(4,128)(2,1)} %bitcast.77), calls=%async_computation | async-start | bytes 917504 | tf_op jit(solution)/shard_map/while/body/eval_jaxpr/all_to_all | solution.py:101
  75.7 0.9 fusion.74
  76.6 10.5 %all-to-all-done = bf16[16,4,3584]{2,1,0:T(4,128)(2,1)S(1)} async-done(((bf16[16,4,3584]{2,1,0:T(4,128)(2,1)}), bf16[16,4,3584]{2,1,0:T(4,128)(2,1)S(1)}, u32[]{:S(2)}, u32[]{:S(2)}) %all-to-all-start) | async-done | bytes 458784 | tf_op jit(solution)/shard_map/while/body/eval_jaxpr/all_to_all | solution.py:101
  87.3 2.8 fusion.73
  90.1 4.6 %convolution_convert_fusion.5 = bf16[64,3584]{1,0:T(8,128)(2,1)S(1)} fusion(bf16[1,512,3584]{2,1,0:T(8,128)(2,1)} %get-tuple-element.450, bf16[64,3584]{1,0:T(8,128)(2,1)S(1)} %reshape.218, bf16[1,3584,512]{2,1,0:T(8,128)(2,1)} %get-tuple-element.449, f32[64,512]{1,0:T(8,128)S(1)} %fusion.73), kind=kOutput, calls=%fused_computation.1.clone.1 | convolution fusion | flops 470188032 | bytes 8388608 | tf_op jit(solution)/shard_map/while/body/eval_jaxpr/dot_general | solution.py:70
  95.6 3.8 %all-to-all-start.1 = ((bf16[16,4,3584]{2,1,0:T(4,128)(2,1)}), bf16[16,4,3584]{2,1,0:T(4,128)(2,1)S(1)}, u32[]{:S(2)}, u32[]{:S(2)}) async-start(bf16[16,4,3584]{2,1,0:T(4,128)(2,1)} %reshape.219), calls=%async_computation.1 | async-start | bytes 917504 | tf_op jit(solution)/shard_map/while/body/eval_jaxpr/all_to_all | solution.py:73
  99.5 13.1 %all-to-all-done.1 = bf16[16,4,3584]{2,1,0:T(4,128)(2,1)S(1)} async-done(((bf16[16,4,3584]{2,1,0:T(4,128)(2,1)}), bf16[16,4,3584]{2,1,0:T(4,128)(2,1)S(1)}, u32[]{:S(2)}, u32[]{:S(2)}) %all-to-all-start.1) | async-done | bytes 458784 | tf_op jit(solution)/shard_map/while/body/eval_jaxpr/all_to_all | solution.py:73
  114.1 4.3 %collective-permute-start = (bf16[8,3584]{1,0:T(8,128)(2,1)S(1)}, bf16[8,3584]{1,0:T(8,128)(2,1)S(1)}, u32[]{:S(2)}, u32[]{:S(2)}) collective-permute-start(bf16[8,3584]{1,0:T(8,128)(2,1)S(1)} %get-tuple-element.401), channel_id=1, source_target_pairs={{0,16},{1,17},{2,18},{3,19},{4,20},{5,21},{6,22},{7,23},{8,24},{9,... | collective-permute-start | bytes 172040 | tf_op jit(solution)/shard_map/while/body/eval_jaxpr/ppermute | solution.py:36
  118.4 1.8 collective-permute-done
  122.3 1.0 fusion.72
  124.3 0.9 broadcast_in_dim.134
  125.2 3.8 %all-to-all-start = ((bf16[16,4,3584]{2,1,0:T(4,128)(2,1)}), bf16[16,4,3584]{2,1,0:T(4,128)(2,1)S(1)}, u32[]{:S(2)}, u32[]{:S(2)}) async-start(bf16[16,4,3584]{2,1,0:T(4,128)(2,1)} %bitcast.77), calls=%async_computation | async-start | bytes 917504 | tf_op jit(solution)/shard_map/while/body/eval_jaxpr/all_to_all | solution.py:101
  130.7 0.9 fusion.74
  131.7 10.5 %all-to-all-done = bf16[16,4,3584]{2,1,0:T(4,128)(2,1)S(1)} async-done(((bf16[16,4,3584]{2,1,0:T(4,128)(2,1)}), bf16[16,4,3584]{2,1,0:T(4,128)(2,1)S(1)}, u32[]{:S(2)}, u32[]{:S(2)}) %all-to-all-start) | async-done | bytes 458784 | tf_op jit(solution)/shard_map/while/body/eval_jaxpr/all_to_all | solution.py:101
  142.3 2.8 fusion.73
  145.1 4.6 %convolution_convert_fusion.5 = bf16[64,3584]{1,0:T(8,128)(2,1)S(1)} fusion(bf16[1,512,3584]{2,1,0:T(8,128)(2,1)} %get-tuple-element.450, bf16[64,3584]{1,0:T(8,128)(2,1)S(1)} %reshape.218, bf16[1,3584,512]{2,1,0:T(8,128)(2,1)} %get-tuple-element.449, f32[64,512]{1,0:T(8,128)S(1)} %fusion.73), kind=kOutput, calls=%fused_computation.1.clone.1 | convolution fusion | flops 470188032 | bytes 8388608 | tf_op jit(solution)/shard_map/while/body/eval_jaxpr/dot_general | solution.py:70
  150.6 3.8 %all-to-all-start.1 = ((bf16[16,4,3584]{2,1,0:T(4,128)(2,1)}), bf16[16,4,3584]{2,1,0:T(4,128)(2,1)S(1)}, u32[]{:S(2)}, u32[]{:S(2)}) async-start(bf16[16,4,3584]{2,1,0:T(4,128)(2,1)} %reshape.219), calls=%async_computation.1 | async-start | bytes 917504 | tf_op jit(solution)/shard_map/while/body/eval_jaxpr/all_to_all | solution.py:73
  154.6 13.1 %all-to-all-done.1 = bf16[16,4,3584]{2,1,0:T(4,128)(2,1)S(1)} async-done(((bf16[16,4,3584]{2,1,0:T(4,128)(2,1)}), bf16[16,4,3584]{2,1,0:T(4,128)(2,1)S(1)}, u32[]{:S(2)}, u32[]{:S(2)}) %all-to-all-start.1) | async-done | bytes 458784 | tf_op jit(solution)/shard_map/while/body/eval_jaxpr/all_to_all | solution.py:73
  169.1 4.3 %collective-permute-start = (bf16[8,3584]{1,0:T(8,128)(2,1)S(1)}, bf16[8,3584]{1,0:T(8,128)(2,1)S(1)}, u32[]{:S(2)}, u32[]{:S(2)}) collective-permute-start(bf16[8,3584]{1,0:T(8,128)(2,1)S(1)} %get-tuple-element.401), channel_id=1, source_target_pairs={{0,16},{1,17},{2,18},{3,19},{4,20},{5,21},{6,22},{7,23},{8,24},{9,... | collective-permute-start | bytes 172040 | tf_op jit(solution)/shard_map/while/body/eval_jaxpr/ppermute | solution.py:36
  173.4 1.8 collective-permute-done
  175.9 21.5 %all-reduce.3.cloned.1.call-done = bf16[2,8,3584]{2,1,0:T(8,128)(2,1)} async-done(((bf16[2,8,3584]{2,1,0:T(8,128)(2,1)}), bf16[2,8,3584]{2,1,0:T(8,128)(2,1)}) %all-reduce.3.cloned.1.call-update) | async-done | bytes 114704 | tf_op jit(solution)/shard_map/psum | solution.py:41
  197.4 3.2 collective-permute-start.1
  200.6 2.7 collective-permute-done.1
  203.3 0.9 pad_maximum_fusion.2
  204.2 1.2 collective-permute-start.2
  205.4 4.9 %collective-permute-done.2 = bf16[2,16,3584]{2,1,0:T(8,128)(2,1)S(1)} collective-permute-done((bf16[2,16,3584]{2,1,0:T(8,128)(2,1)S(1)}, bf16[2,16,3584]{2,1,0:T(8,128)(2,1)S(1)}, u32[]{:S(2)}, u32[]{:S(2)}) %collective-permute-start.2) | collective-permute-done | bytes 229408 | tf_op jit(solution)/shard_map/ppermute | solution.py:17
  210.3 0.9 pad_maximum_fusion.1
  212.1 0.9 constant_dynamic-update-slice_fusion.9
  213.0 11.1 %collective-permute-done.3 = bf16[2,32,3584]{2,1,0:T(8,128)(2,1)S(1)} collective-permute-done((bf16[2,32,3584]{2,1,0:T(8,128)(2,1)S(1)}, bf16[2,32,3584]{2,1,0:T(8,128)(2,1)S(1)}, u32[]{:S(2)}, u32[]{:S(2)}) %collective-permute-start.3) | collective-permute-done | bytes 458784 | tf_op jit(solution)/shard_map/ppermute | solution.py:17
  224.2 1.0 pad_maximum_fusion
  225.1 1.5 collective-permute-start.4
  226.7 41.6 %collective-permute-done.4 = bf16[2,64,3584]{2,1,0:T(8,128)(2,1)S(1)} collective-permute-done((bf16[2,64,3584]{2,1,0:T(8,128)(2,1)S(1)}, bf16[2,64,3584]{2,1,0:T(8,128)(2,1)S(1)}, u32[]{:S(2)}, u32[]{:S(2)}) %collective-permute-start.4) | collective-permute-done | bytes 917536 | tf_op jit(solution)/shard_map/ppermute | solution.py:17
  269.9 37.3 %pmax.7 = f32[2,128]{1,0:T(2,128)S(1)} all-reduce(f32[2,128]{1,0:T(2,128)S(1)} %get-tuple-element.314), channel_id=1, replica_groups=mesh['section'=2,'expert'=16] {'section','expert'}, use_global_device_ids=true, to_apply=%region_15.16 | all-reduce | flops 256 | bytes 2048 | tf_op jit(solution)/shard_map/pmax | solution.py:142
  307.4 41.5 %all-reduce = (f32[2,128]{1,0:T(2,128)S(1)}, f32[2,128]{1,0:T(2,128)S(1)}) all-reduce(f32[2,128]{1,0:T(2,128)S(1)} %get-tuple-element.279, f32[2,128]{1,0:T(2,128)S(1)} %get-tuple-element.278), channel_id=1, replica_groups=mesh['section'=2,'expert'=16] {'section','expert'}, use_global_device_ids=true, to_apply=%region_13.14 | all-reduce | flops 512 | bytes 4096 | tf_op jit(solution)/shard_map/psum | solution.py:144
  (136 shorter events, 27.0 us)
Async XLA Ops:
  7.2 261.9 %copy-start = (bf16[256,3584]{1,0:T(8,128)(2,1)S(1)}, bf16[256,3584]{1,0:T(8,128)(2,1)}, u32[]{:S(2)}) copy-start(bf16[256,3584]{1,0:T(8,128)(2,1)} %param.20) | copy-start | bytes 5505028
  7.2 190.2 %all-reduce.3.cloned.1.call-start = ((), (), s32[]{:S(2)}) async-start(), calls=%async_computation.2 | async-start | bytes 229376 | tf_op jit(solution)/shard_map/psum | solution.py:41
  12.4 20.6 %all-to-all-start = ((bf16[16,4,3584]{2,1,0:T(4,128)(2,1)}), bf16[16,4,3584]{2,1,0:T(4,128)(2,1)S(1)}, u32[]{:S(2)}, u32[]{:S(2)}) async-start(bf16[16,4,3584]{2,1,0:T(4,128)(2,1)} %bitcast.77), calls=%async_computation | async-start | bytes 917504 | tf_op jit(solution)/shard_map/while/body/eval_jaxpr/all_to_all | solution.py:101
  41.4 17.0 %all-to-all-start.1 = ((bf16[16,4,3584]{2,1,0:T(4,128)(2,1)}), bf16[16,4,3584]{2,1,0:T(4,128)(2,1)S(1)}, u32[]{:S(2)}, u32[]{:S(2)}) async-start(bf16[16,4,3584]{2,1,0:T(4,128)(2,1)} %reshape.219), calls=%async_computation.1 | async-start | bytes 917504 | tf_op jit(solution)/shard_map/while/body/eval_jaxpr/all_to_all | solution.py:73
  59.9 5.2 %collective-permute-start = (bf16[8,3584]{1,0:T(8,128)(2,1)S(1)}, bf16[8,3584]{1,0:T(8,128)(2,1)S(1)}, u32[]{:S(2)}, u32[]{:S(2)}) collective-permute-start(bf16[8,3584]{1,0:T(8,128)(2,1)S(1)} %get-tuple-element.401), channel_id=1, source_target_pairs={{0,16},{1,17},{2,18},{3,19},{4,20},{5,21},{6,22},{7,23},{8,24},{9,... | collective-permute-start | bytes 172040 | tf_op jit(solution)/shard_map/while/body/eval_jaxpr/ppermute | solution.py:36
  70.1 17.0 %all-to-all-start = ((bf16[16,4,3584]{2,1,0:T(4,128)(2,1)}), bf16[16,4,3584]{2,1,0:T(4,128)(2,1)S(1)}, u32[]{:S(2)}, u32[]{:S(2)}) async-start(bf16[16,4,3584]{2,1,0:T(4,128)(2,1)} %bitcast.77), calls=%async_computation | async-start | bytes 917504 | tf_op jit(solution)/shard_map/while/body/eval_jaxpr/all_to_all | solution.py:101
  95.6 17.0 %all-to-all-start.1 = ((bf16[16,4,3584]{2,1,0:T(4,128)(2,1)}), bf16[16,4,3584]{2,1,0:T(4,128)(2,1)S(1)}, u32[]{:S(2)}, u32[]{:S(2)}) async-start(bf16[16,4,3584]{2,1,0:T(4,128)(2,1)} %reshape.219), calls=%async_computation.1 | async-start | bytes 917504 | tf_op jit(solution)/shard_map/while/body/eval_jaxpr/all_to_all | solution.py:73
  114.1 6.1 %collective-permute-start = (bf16[8,3584]{1,0:T(8,128)(2,1)S(1)}, bf16[8,3584]{1,0:T(8,128)(2,1)S(1)}, u32[]{:S(2)}, u32[]{:S(2)}) collective-permute-start(bf16[8,3584]{1,0:T(8,128)(2,1)S(1)} %get-tuple-element.401), channel_id=1, source_target_pairs={{0,16},{1,17},{2,18},{3,19},{4,20},{5,21},{6,22},{7,23},{8,24},{9,... | collective-permute-start | bytes 172040 | tf_op jit(solution)/shard_map/while/body/eval_jaxpr/ppermute | solution.py:36
  125.2 17.0 %all-to-all-start = ((bf16[16,4,3584]{2,1,0:T(4,128)(2,1)}), bf16[16,4,3584]{2,1,0:T(4,128)(2,1)S(1)}, u32[]{:S(2)}, u32[]{:S(2)}) async-start(bf16[16,4,3584]{2,1,0:T(4,128)(2,1)} %bitcast.77), calls=%async_computation | async-start | bytes 917504 | tf_op jit(solution)/shard_map/while/body/eval_jaxpr/all_to_all | solution.py:101
  150.6 17.0 %all-to-all-start.1 = ((bf16[16,4,3584]{2,1,0:T(4,128)(2,1)}), bf16[16,4,3584]{2,1,0:T(4,128)(2,1)S(1)}, u32[]{:S(2)}, u32[]{:S(2)}) async-start(bf16[16,4,3584]{2,1,0:T(4,128)(2,1)} %reshape.219), calls=%async_computation.1 | async-start | bytes 917504 | tf_op jit(solution)/shard_map/while/body/eval_jaxpr/all_to_all | solution.py:73
  169.1 6.1 %collective-permute-start = (bf16[8,3584]{1,0:T(8,128)(2,1)S(1)}, bf16[8,3584]{1,0:T(8,128)(2,1)S(1)}, u32[]{:S(2)}, u32[]{:S(2)}) collective-permute-start(bf16[8,3584]{1,0:T(8,128)(2,1)S(1)} %get-tuple-element.401), channel_id=1, source_target_pairs={{0,16},{1,17},{2,18},{3,19},{4,20},{5,21},{6,22},{7,23},{8,24},{9,... | collective-permute-start | bytes 172040 | tf_op jit(solution)/shard_map/while/body/eval_jaxpr/ppermute | solution.py:36
  197.4 71.0 %copy-start.1 = (bf16[2,8,3584]{2,1,0:T(8,128)(2,1)S(1)}, bf16[2,8,3584]{2,1,0:T(8,128)(2,1)}, u32[]{:S(2)}) copy-start(bf16[2,8,3584]{2,1,0:T(8,128)(2,1)} %all-reduce.3.cloned.1.call-done) | copy-start | bytes 344068
  197.4 5.9 %collective-permute-start.1 = (bf16[2,8,3584]{2,1,0:T(8,128)(2,1)}, bf16[2,8,3584]{2,1,0:T(8,128)(2,1)S(1)}, u32[]{:S(2)}, u32[]{:S(2)}) collective-permute-start(bf16[2,8,3584]{2,1,0:T(8,128)(2,1)} %all-reduce.3.cloned.1.call-done), channel_id=1, source_target_pairs={{0,15},{1,0},{2,1},{3,2},{4,3},{5,4},{6,5},{7,6},{8,7},{9,8},{10,9... | collective-permute-start | bytes 344072 | tf_op jit(solution)/shard_map/ppermute | solution.py:17
  204.2 6.1 %collective-permute-start.2 = (bf16[2,16,3584]{2,1,0:T(8,128)(2,1)S(1)}, bf16[2,16,3584]{2,1,0:T(8,128)(2,1)S(1)}, u32[]{:S(2)}, u32[]{:S(2)}) collective-permute-start(bf16[2,16,3584]{2,1,0:T(8,128)(2,1)S(1)} %pad_maximum_fusion.2), channel_id=1, source_target_pairs={{0,14},{1,15},{2,0},{3,1},{4,2},{5,3},{6,4},{7,5},{8,6},{9,7},{10,... | collective-permute-start | bytes 688136 | tf_op jit(solution)/shard_map/ppermute | solution.py:17
  211.2 12.9 %collective-permute-start.3 = (bf16[2,32,3584]{2,1,0:T(8,128)(2,1)S(1)}, bf16[2,32,3584]{2,1,0:T(8,128)(2,1)S(1)}, u32[]{:S(2)}, u32[]{:S(2)}) collective-permute-start(bf16[2,32,3584]{2,1,0:T(8,128)(2,1)S(1)} %pad_maximum_fusion.1), channel_id=1, source_target_pairs={{0,12},{1,13},{2,14},{3,15},{4,0},{5,1},{6,2},{7,3},{8,4},{9,5},{1... | collective-permute-start | bytes 1376264 | tf_op jit(solution)/shard_map/ppermute | solution.py:17
  225.1 43.2 %collective-permute-start.4 = (bf16[2,64,3584]{2,1,0:T(8,128)(2,1)S(1)}, bf16[2,64,3584]{2,1,0:T(8,128)(2,1)S(1)}, u32[]{:S(2)}, u32[]{:S(2)}) collective-permute-start(bf16[2,64,3584]{2,1,0:T(8,128)(2,1)S(1)} %pad_maximum_fusion), channel_id=1, source_target_pairs={{0,8},{1,9},{2,10},{3,11},{4,12},{5,13},{6,14},{7,15},{8,0},{9,1},... | collective-permute-start | bytes 2752520 | tf_op jit(solution)/shard_map/ppermute | solution.py:17
  226.7 42.4 %copy-start.4 = (f32[3584]{0:T(1024)S(1)}, f32[3584]{0:T(1024)}, u32[]{:S(2)}) copy-start(f32[3584]{0:T(1024)} %param.19) | copy-start | bytes 43012
  268.6 38.6 %copy-start.2 = (s32[2,128]{1,0:T(2,128)S(1)}, s32[2,128]{1,0:T(2,128)}, u32[]{:S(2)}) copy-start(s32[2,128]{1,0:T(2,128)} %param.22) | copy-start | bytes 3076
  268.6 80.4 %copy-start.3 = (s32[2,128]{1,0:T(2,128)S(1)}, s32[2,128]{1,0:T(2,128)}, u32[]{:S(2)}) copy-start(s32[2,128]{1,0:T(2,128)} %param.23) | copy-start | bytes 3076
Sparse Core Ops, SparseCore 0:
  176.0 21.3 all-reduce.2
